TPU v7x, 32 devices: a whole 2x2x4 slice. The times are simulated.
32 devices in a mesh: freq: 8 (over z, x), sens: 4 (over y, core).
Axes of the slice: x: 2, y: 2, z: 4, core: 2. Of those that a mesh axis runs over, the one named last changes fastest.
Arguments:
- samples: bfloat16 [128, 608, 420], P('freq', 'sens'), may hold values from -6 to 6
- response_tiles: bfloat16 [448, 2, 608, 21], P('freq', None, 'sens'), may hold values from -0.25 to 0.25
- slot_sensor: int32 [608], P('sens'), may hold values from -1 to 599, as said below
- sensor_noise: float32 [600], replicated, may hold values from 0.02 to 5
- advance_offset: int32 [21], replicated, may hold values from 0 to 419
Outputs:
- outlook_values: bfloat16 [128, 21, 420], P('freq')
- noise_spread: float32 [21], replicated
Inputs may be any that keep to these rules, and one draw needn't show every extreme that they name: `slot_sensor`: every sensor number appears in exactly one slot; the other 8 slots hold -1.
All inputs are finite; a program needn't handle non-finite values.
Results may differ from a plain program's by a relative error of at most 0.0055.
Values may be sent and summed in bfloat16 or wider, within the bound.
A program may use at most 64 MiB of HBM per device.

v0:
```python
import math
import jax
import jax.numpy as jnp
from jax import lax
from jax.sharding import PartitionSpec as P

KEPT_HARMONICS = 448


def angles(first_bin, bin_count, period, factor):
    bin_index = first_bin + lax.iota(jnp.int32, bin_count)
    turn_count = bin_index[:, None] * factor[None, :] % period
    return turn_count.astype(jnp.float32) * (2.0 * math.pi / period)


def forward_table(bin_count, step_count, period):
    phase_angle = angles(0, bin_count, period, lax.iota(jnp.int32, step_count))
    return jnp.stack([jnp.cos(phase_angle), -jnp.sin(phase_angle)]).astype(jnp.bfloat16)


def inverse_table(bin_count, step_count, period):
    bin_index = lax.iota(jnp.int32, bin_count)
    weight = jnp.where(bin_index == 0, 1.0, 2.0).astype(jnp.float32) / period
    phase_angle = angles(0, bin_count, period, lax.iota(jnp.int32, step_count))
    return jnp.stack(
        [weight[:, None] * jnp.cos(phase_angle), -weight[:, None] * jnp.sin(phase_angle)]
    )


def contract(spectra, blocks):

    def product(left, right):
        return jnp.einsum("krs,ksq->kqr", left, right, preferred_element_type=jnp.float32)

    real_part = product(spectra[0], blocks[:, 0]) - product(spectra[1], blocks[:, 1])
    imag_part = product(spectra[0], blocks[:, 1]) + product(spectra[1], blocks[:, 0])
    return jnp.stack([real_part, imag_part])


def rotate(summed, first_bin, advance_offset, period):
    twiddle = angles(first_bin, summed.shape[1], period, advance_offset)[:, :, None]
    cosine = jnp.cos(twiddle)
    sine_part = jnp.sin(twiddle)
    real_part = summed[0] * cosine - summed[1] * sine_part
    imag_part = summed[0] * sine_part + summed[1] * cosine
    return jnp.stack([real_part, imag_part])


def on_device(samples, response_tiles, slot_sensor, sensor_noise, advance_offset):
    highest = lax.Precision.HIGHEST
    bins_dev = response_tiles.shape[0]
    first_bin = lax.axis_index("freq") * bins_dev
    period = 2 * KEPT_HARMONICS
    step_count = samples.shape[2]
    live_slot = (slot_sensor >= 0).astype(jnp.bfloat16)
    blocks = response_tiles * live_slot[None, None, :, None]
    sensor_ids = lax.iota(jnp.int32, sensor_noise.shape[0])
    slot_noise = jnp.sum(
        jnp.where(
            slot_sensor[:, None] == sensor_ids[None, :], sensor_noise[None, :], jnp.float32(0.0)
        ),
        axis=1,
    )
    wide = blocks.astype(jnp.float32)
    power = wide[:, 0] * wide[:, 0] + wide[:, 1] * wide[:, 1]
    bin_index = first_bin + lax.iota(jnp.int32, bins_dev)
    bin_weight = jnp.where(bin_index == 0, 1.0, 2.0).astype(jnp.float32) / period
    per_bin = jnp.einsum("ksq,s->kq", power, slot_noise, precision=highest)
    noise_spread = lax.psum(jnp.dot(bin_weight, per_bin, precision=highest), ("freq", "sens"))
    forward = forward_table(KEPT_HARMONICS, step_count, period)
    spectra = jnp.einsum(
        "rst,ckt->ckrs", samples, forward, preferred_element_type=jnp.float32
    ).astype(jnp.bfloat16)
    partial_value = contract(spectra, lax.all_gather(blocks, "freq", axis=0, tiled=True))
    base_bin = 0
    backward = inverse_table(KEPT_HARMONICS, step_count, period)
    summed = lax.psum(partial_value, "sens")
    shifted = rotate(summed, base_bin, advance_offset, period)
    kept_entries_local = jnp.einsum("ckqr,ckt->rqt", shifted, backward, precision=highest)
    outlook_values = kept_entries_local.astype(jnp.bfloat16)
    return (outlook_values, noise_spread)


def solution(mesh):
    placed = (P("freq", "sens", None), P("freq", None, "sens", None), P("sens"), P(), P())
    return jax.shard_map(
        on_device,
        mesh=mesh,
        in_specs=placed,
        out_specs=(P("freq", None, None), P()),
        check_vma=False,
    )
```

profile of v0, /device:TPU:0, one launch (start us, length us, event | category | flops | bytes accessed | tf_op | source)
XLA Modules:
  0.0 256.4 jit_solution(4376142394990606409)
XLA Ops:
  7.2 0.0 copy-start
  7.2 0.0 all-gather.2.cloned.1.call-start
  7.2 0.8 compare_convert_fusion
  8.1 0.0 copy-start.4
  8.1 0.0 copy-start.5
  8.1 3.6 %fusion.59 = (f32[56,2,152,21]{2,3,0,1:T(8,128)}, bf16[56,2,152,21]{2,3,0,1:T(8,128)(2,1)}) fusion(bf16[152]{0:T(256)(128)(2,1)S(1)} %compare_convert_fusion, bf16[56,2,152,21]{2,1,3,0:T(2,128)(2,1)} %param.6), kind=kLoop, calls=%fused_computation.80 | loop fusion | flops 715008 | bytes 2860336 | tf_op jit(solution)/shard_map/convert_element_type | solution.py:64
  11.7 0.0 all-gather.2.cloned.1.call-update
  11.7 0.0 all-reduce.2.cloned.1.call-start
  11.8 0.0 copy-done.4
  11.8 0.0 copy-done.5
  11.8 0.2 select_reduce_fusion
  12.0 1.9 fusion.10
  13.9 1.9 fusion.17
  15.8 0.1 copy.35
  15.9 0.1 convolution_bitcast_fusion
  16.1 45.9 %psum.15 = f32[21]{0:T(128)} all-reduce(f32[21]{0:T(128)S(1)} %convolution_bitcast_fusion), channel_id=1, replica_groups=mesh['freq'=8,'sens'=4] {'freq','sens'}, use_global_device_ids=true, to_apply=%region_2.3 | all-reduce | flops 21 | bytes 168 | tf_op jit(solution)/shard_map/psum | solution.py:69
  62.0 3.8 %negate_convert_fusion = (bf16[1,448,420]{1,2,0:T(8,128)(2,1)S(1)}, bf16[1,448,420]{1,2,0:T(8,128)(2,1)S(1)}) fusion(), kind=kLoop, calls=%fused_computation.36 | loop fusion | flops 2257920 | bytes 752640 | tf_op jit(solution)/shard_map/convert.1
  65.8 0.0 copy-done
  65.8 2.9 %convolution_convert_fusion = bf16[2,448,16,152]{1,3,2,0:T(8,128)(2,1)S(1)} fusion(bf16[16,152,420]{2,1,0:T(8,128)(2,1)S(1)} %copy-done, bf16[1,448,420]{1,2,0:T(8,128)(2,1)S(1)} %get-tuple-element.16, bf16[1,448,420]{1,2,0:T(8,128)(2,1)S(1)} %get-tuple-element.17), kind=kOutput, calls=%fused_computation.8 | convolution fusion | flops 1834104832 | bytes 7153664 | tf_op jit(solution)/shard_map/rst,ckt->ckrs/dot_general | solution.py:71
  68.7 2.6 %slice_bitcast_fusion.7 = (bf16[448,16,152]{0,2,1:T(8,128)(2,1)}, bf16[448,16,152]{0,2,1:T(8,128)(2,1)}) fusion(bf16[2,448,16,152]{1,3,2,0:T(8,128)(2,1)S(1)} %convolution_convert_fusion), kind=kLoop, calls=%fused_computation.10 | loop fusion | bytes 8716288 | tf_op jit(solution)/shard_map/squeeze | solution.py:35
  71.3 7.4 %copy.24 = bf16[448,16,152]{2,1,0:T(8,128)(2,1)} copy(bf16[448,16,152]{0,2,1:T(8,128)(2,1)} %get-tuple-element.8) | data formatting | bytes 4358144 | tf_op jit(solution)/shard_map/squeeze | solution.py:35
  78.8 7.5 %copy.25 = bf16[448,16,152]{2,1,0:T(8,128)(2,1)} copy(bf16[448,16,152]{0,2,1:T(8,128)(2,1)} %get-tuple-element.9) | data formatting | bytes 4358144 | tf_op jit(solution)/shard_map/squeeze | solution.py:35
  86.3 86.1 %all-gather.2.cloned.1.call-done = bf16[448,2,152,21]{2,3,0,1:T(8,128)(2,1)} async-done(((bf16[56,2,152,21]{2,3,0,1:T(8,128)(2,1)}), bf16[448,2,152,21]{2,3,0,1:T(8,128)(2,1)}) %all-gather.2.cloned.1.call-update) | async-done | bytes 5720080 | tf_op jit(solution)/shard_map/all_gather | solution.py:74
  172.4 0.0 copy-start.1
  172.4 5.3 %fusion = f32[448,21,16]{1,2,0:T(8,128)S(1)} fusion(bf16[448,16,152]{2,1,0:T(8,128)(2,1)} %copy.25, bf16[448,2,152,21]{2,3,0,1:T(8,128)(2,1)} %all-gather.2.cloned.1.call-done), kind=kOutput, calls=%fused_computation.2 | convolution fusion | flops 45760512 | bytes 9777152 | tf_op jit(solution)/shard_map/krs,ksq->kqr/dot_general | solution.py:33
  177.8 1.4 copy-done.1
  179.2 5.5 %add_bitcast_fusion = f32[1,448,21,16]{2,3,1,0:T(8,128)} fusion(f32[448,21,16]{1,2,0:T(8,128)S(1)} %fusion, bf16[448,16,152]{2,1,0:T(8,128)(2,1)} %copy.24, bf16[448,2,152,21]{2,3,0,1:T(8,128)(2,1)S(1)} %copy-done.1), kind=kOutput, calls=%fused_computation.6 | convolution fusion | flops 45911040 | bytes 11956224 | tf_op jit(solution)/shard_map/krs,ksq->kqr/dot_general | solution.py:33
  184.7 3.0 %copy.29 = f32[1,448,21,16]{1,3,2,0:T(8,128)S(1)} copy(f32[1,448,21,16]{2,3,1,0:T(8,128)} %add_bitcast_fusion) | data formatting | bytes 1204224 | tf_op jit(solution)/shard_map/stack | solution.py:37
  187.7 0.0 copy-start.2
  187.7 5.3 %fusion.1 = f32[448,21,16]{1,2,0:T(8,128)S(1)} fusion(bf16[448,16,152]{2,1,0:T(8,128)(2,1)} %copy.24, bf16[448,2,152,21]{2,3,0,1:T(8,128)(2,1)} %all-gather.2.cloned.1.call-done), kind=kOutput, calls=%fused_computation.3 | convolution fusion | flops 45760512 | bytes 9777152 | tf_op jit(solution)/shard_map/krs,ksq->kqr/dot_general | solution.py:33
  193.0 0.0 copy-done.2
  193.0 6.1 %subtract_bitcast_fusion = f32[1,448,21,16]{2,3,1,0:T(8,128)} fusion(f32[448,21,16]{1,2,0:T(8,128)S(1)} %fusion.1, bf16[448,16,152]{2,1,0:T(8,128)(2,1)S(1)} %copy-done.2, bf16[448,2,152,21]{2,3,0,1:T(8,128)(2,1)} %all-gather.2.cloned.1.call-done), kind=kOutput, calls=%fused_computation.7 | convolution fusion | flops 45911040 | bytes 8888320 | tf_op jit(solution)/shard_map/krs,ksq->kqr/dot_general | solution.py:33
  199.2 3.7 %copy.28 = f32[1,448,21,16]{1,3,2,0:T(8,128)} copy(f32[1,448,21,16]{2,3,1,0:T(8,128)} %subtract_bitcast_fusion) | data formatting | bytes 1204224 | tf_op jit(solution)/shard_map/stack | solution.py:37
  202.8 0.0 copy-start.6
  202.8 2.4 pad_maximum_fusion
  205.2 0.0 all-reduce.2.cloned.1.call-update
  205.2 0.0 copy-done.6
  205.2 0.3 fusion.39
  205.5 4.5 %fusion.31 = (f32[1,448,420]{1,2,0:T(8,128)S(1)}, f32[1,448,420]{1,2,0:T(8,128)}) fusion(f32[448]{0:T(512)S(1)} %select_multiply_fusion, f32[448]{0:T(512)S(1)} %fusion.42), kind=kLoop, calls=%fused_computation.43 | loop fusion | flops 2069760 | bytes 1508864 | tf_op jit(solution)/shard_map/mul | solution.py:26
  210.0 33.6 %all-reduce.2.cloned.1.call-done = f32[2,448,21,16]{1,3,2,0:T(8,128)} async-done(((f32[2,448,21,16]{1,3,2,0:T(8,128)}), f32[2,448,21,16]{1,3,2,0:T(8,128)}) %all-reduce.2.cloned.1.call-update) | async-done | bytes 1204240 | tf_op jit(solution)/shard_map/psum | solution.py:77
  243.6 0.0 copy-start.3
  243.6 1.6 multiply_subtract_fusion
  245.2 0.1 pad_maximum_fusion.1
  245.3 0.0 copy-done.3
  245.3 3.4 %fusion.19 = bf16[16,21,420]{2,1,0:T(8,128)(2,1)S(1)} fusion(f32[2,448,21,16]{1,3,2,0:T(8,128)S(1)} %pad_maximum_fusion.1, f32[1,448,420]{1,2,0:T(8,128)S(1)} %copy-done.3, f32[1,448,420]{1,2,0:T(8,128)S(1)} %get-tuple-element.18), kind=kOutput, calls=%fused_computation.29 | convolution fusion | flops 1517839616 | bytes 2991744 | tf_op jit(solution)/shard_map/ckqr,ckt->rqt/dot_general | solution.py:79
  248.7 0.8 copy.31
  (2 shorter events, 0.0 us)
Async XLA Ops:
  7.2 58.6 %copy-start = (bf16[16,152,420]{2,1,0:T(8,128)(2,1)S(1)}, bf16[16,152,420]{2,1,0:T(8,128)(2,1)}, u32[]{:S(2)}) copy-start(bf16[16,152,420]{2,1,0:T(8,128)(2,1)} %param.5) | copy-start | bytes 6128644
  7.2 165.2 %all-gather.2.cloned.1.call-start = ((), (), s32[]{:S(2)}) async-start(), calls=%async_computation | async-start | bytes 12386304 | tf_op jit(solution)/shard_map/all_gather | solution.py:74
  8.1 3.7 %copy-start.4 = (f32[600]{0:T(1024)S(1)}, f32[600]{0:T(1024)}, u32[]{:S(2)}) copy-start(f32[600]{0:T(1024)} %param.8) | copy-start | bytes 7204
  8.1 3.7 %copy-start.5 = (s32[152]{0:T(256)S(1)}, s32[152]{0:T(256)}, u32[]{:S(2)}) copy-start(s32[152]{0:T(256)} %param.7) | copy-start | bytes 1828
  11.7 231.8 %all-reduce.2.cloned.1.call-start = ((), (), s32[]{:S(2)}) async-start(), calls=%async_computation.1 | async-start | bytes 2752512 | tf_op jit(solution)/shard_map/psum | solution.py:77
  172.4 6.8 %copy-start.1 = (bf16[448,2,152,21]{2,3,0,1:T(8,128)(2,1)S(1)}, bf16[448,2,152,21]{2,3,0,1:T(8,128)(2,1)}, u32[]{:S(2)}) copy-start(bf16[448,2,152,21]{2,3,0,1:T(8,128)(2,1)} %all-gather.2.cloned.1.call-done) | copy-start | bytes 17160196
  187.7 5.4 %copy-start.2 = (bf16[448,16,152]{2,1,0:T(8,128)(2,1)S(1)}, bf16[448,16,152]{2,1,0:T(8,128)(2,1)}, u32[]{:S(2)}) copy-start(bf16[448,16,152]{2,1,0:T(8,128)(2,1)} %copy.25) | copy-start | bytes 6537220
  202.8 2.4 copy-start.6
  243.6 1.7 copy-start.3
Sparse Core Ops, SparseCore 0:
  11.9 160.5 all-gather.1
  205.3 38.1 all-reduce.1
where the time goes:
time: 257 us; the launch traced here: 256 us
  waiting for transfers between devices  120 us (47%)
  blocking collectives  45.9 us (18%)
  matrix products  30.6 us (12%)
  local copies, waits for them, and re-layouts  26.6 us (10%)
  other arithmetic  19.2 us (7%)
  between operations  14.2 us (6%)
    all_gather x1, waiting for transfers between devices, on_device(): lax.all_gather(blocks, 'freq', axis=0, tiled=True)  86.1 us
    psum x1, blocking collectives, on_device(): lax.psum(jnp.dot(bin_weight, per_bin, precision=highest), ('freq', 'sens'))  45.9 us
    psum x1, waiting for transfers between devices, on_device(): summed = lax.psum(partial_value, 'sens')  33.6 us
    dot_general x4, matrix products, product(): jnp.einsum('krs,ksq->kqr', left, right, preferred_element_type=jnp.float32)  22.3 us
    squeeze x2, local copies, waits for them, and re-layouts, contract(): spectra[0]  10 us
    squeeze x1, local copies, waits for them, and re-layouts, contract(): spectra[1]  7.52 us
    another operation x2, local copies, waits for them, and re-layouts, contract(): return jnp.stack([real_part, imag_part])  6.64 us
  transfers between devices with their start and end apart: 2, of which 2 were waited for; matrix products, arithmetic and copies ran while one was open for 13% of the time, Pallas kernels for 0%

commit v1 on v0

--- a/solution.py
+++ b/solution.py
@@ -74,7 +74,10 @@
     partial_value = contract(spectra, lax.all_gather(blocks, "freq", axis=0, tiled=True))
     base_bin = 0
     backward = inverse_table(KEPT_HARMONICS, step_count, period)
-    summed = lax.psum(partial_value, "sens")
+    size, summed = (lax.axis_size("sens"), partial_value)
+    for reach in [1 << k for k in range(size.bit_length() - 1)]:
+        swap = [(i, i ^ reach) for i in range(size)]
+        summed = summed + lax.ppermute(summed, "sens", swap)
     shifted = rotate(summed, base_bin, advance_offset, period)
     kept_entries_local = jnp.einsum("ckqr,ckt->rqt", shifted, backward, precision=highest)
     outlook_values = kept_entries_local.astype(jnp.bfloat16)

time: 257 us -> 294 us (1.14)
  waiting for transfers between devices: 120 us -> 137 us
  blocking collectives: 45.9 us -> 61 us
    all_gather x1, waiting for transfers between devices: 86.1 us -> 135 us  [on_device(): lax.all_gather(blocks, 'freq', axis=0, tiled=True)]
    psum x1 -> x0, waiting for transfers between devices: 33.6 us -> none  [on_device(): summed = lax.psum(partial_value, 'sens')]
    psum x1, blocking collectives: 45.9 us -> 61 us  [on_device(): lax.psum(jnp.dot(bin_weight, per_bin, precision=highest), ('freq', 'sens'))]
    add x0 -> x2, other arithmetic: none -> 5.13 us  [on_device(): summed = summed + lax.ppermute(summed, 'sens', swap)]
  transfers between devices with their start and end apart: 2 -> 3, of which waited for: 2 -> 2; matrix products, arithmetic and copies ran while one was open for 13% -> 11% of each run, Pallas kernels for 0% -> 0%
where the time goes in v1:
time: 294 us; the launch traced here: 293 us
  waiting for transfers between devices  137 us (47%)
  blocking collectives  61 us (21%)
  matrix products  30.7 us (10%)
  local copies, waits for them, and re-layouts  26.7 us (9%)
  other arithmetic  22.1 us (8%)
  between operations  14.2 us (5%)
    all_gather x1, waiting for transfers between devices, on_device(): lax.all_gather(blocks, 'freq', axis=0, tiled=True)  135 us
    psum x1, blocking collectives, on_device(): lax.psum(jnp.dot(bin_weight, per_bin, precision=highest), ('freq', 'sens'))  61 us
    dot_general x4, matrix products, product(): jnp.einsum('krs,ksq->kqr', left, right, preferred_element_type=jnp.float32)  22.3 us
    squeeze x2, local copies, waits for them, and re-layouts, contract(): spectra[0]  10.2 us
    squeeze x1, local copies, waits for them, and re-layouts, contract(): spectra[1]  7.42 us
    another operation x2, local copies, waits for them, and re-layouts, contract(): return jnp.stack([real_part, imag_part])  6.66 us
  transfers between devices with their start and end apart: 3, of which 2 were waited for; matrix products, arithmetic and copies ran while one was open for 11% of the time, Pallas kernels for 0%

profile of v1, /device:TPU:0, one launch (start us, length us, event | category | flops | bytes accessed | tf_op | source)
XLA Modules:
  0.0 293.0 jit_solution(11452340311349033262)
XLA Ops:
  7.2 0.0 copy-start
  7.2 0.0 all-gather.2.cloned.1.call-start
  7.2 0.8 compare_convert_fusion
  8.1 3.5 %fusion.59 = (f32[56,2,152,21]{2,3,0,1:T(8,128)}, bf16[56,2,152,21]{2,3,0,1:T(8,128)(2,1)}) fusion(bf16[152]{0:T(256)(128)(2,1)S(1)} %compare_convert_fusion, bf16[56,2,152,21]{2,1,3,0:T(2,128)(2,1)} %param.6), kind=kLoop, calls=%fused_computation.80 | loop fusion | flops 715008 | bytes 2860336 | tf_op jit(solution)/shard_map/convert_element_type | solution.py:64
  11.6 0.0 all-gather.2.cloned.1.call-update
  11.6 3.8 %negate_convert_fusion = (bf16[1,448,420]{1,2,0:T(8,128)(2,1)S(1)}, bf16[1,448,420]{1,2,0:T(8,128)(2,1)S(1)}) fusion(), kind=kLoop, calls=%fused_computation.36 | loop fusion | flops 2257920 | bytes 752640 | tf_op jit(solution)/shard_map/convert.1
  15.4 0.0 copy-done
  15.4 2.9 %convolution_convert_fusion = bf16[2,448,16,152]{1,3,2,0:T(8,128)(2,1)S(1)} fusion(bf16[16,152,420]{2,1,0:T(8,128)(2,1)S(1)} %copy-done, bf16[1,448,420]{1,2,0:T(8,128)(2,1)S(1)} %get-tuple-element.16, bf16[1,448,420]{1,2,0:T(8,128)(2,1)S(1)} %get-tuple-element.17), kind=kOutput, calls=%fused_computation.8 | convolution fusion | flops 1834104832 | bytes 7153664 | tf_op jit(solution)/shard_map/rst,ckt->ckrs/dot_general | solution.py:71
  18.3 2.6 slice_bitcast_fusion.7
  20.9 7.6 %copy.24 = bf16[448,16,152]{2,1,0:T(8,128)(2,1)} copy(bf16[448,16,152]{0,2,1:T(8,128)(2,1)} %get-tuple-element.8) | data formatting | bytes 4358144 | tf_op jit(solution)/shard_map/squeeze | solution.py:35
  28.5 7.4 %copy.25 = bf16[448,16,152]{2,1,0:T(8,128)(2,1)} copy(bf16[448,16,152]{0,2,1:T(8,128)(2,1)} %get-tuple-element.9) | data formatting | bytes 4358144 | tf_op jit(solution)/shard_map/squeeze | solution.py:35
  35.9 135.4 %all-gather.2.cloned.1.call-done = bf16[448,2,152,21]{2,3,0,1:T(8,128)(2,1)} async-done(((bf16[56,2,152,21]{2,3,0,1:T(8,128)(2,1)}), bf16[448,2,152,21]{2,3,0,1:T(8,128)(2,1)}) %all-gather.2.cloned.1.call-update) | async-done | bytes 5720080 | tf_op jit(solution)/shard_map/all_gather | solution.py:74
  171.4 0.0 copy-start.1
  171.4 5.3 %fusion = f32[448,21,16]{1,2,0:T(8,128)S(1)} fusion(bf16[448,16,152]{2,1,0:T(8,128)(2,1)} %copy.25, bf16[448,2,152,21]{2,3,0,1:T(8,128)(2,1)} %all-gather.2.cloned.1.call-done), kind=kOutput, calls=%fused_computation.2 | convolution fusion | flops 45760512 | bytes 9777152 | tf_op jit(solution)/shard_map/krs,ksq->kqr/dot_general | solution.py:33
  176.7 1.4 copy-done.1
  178.2 5.5 %add_bitcast_fusion = f32[1,448,21,16]{2,3,1,0:T(8,128)} fusion(f32[448,21,16]{1,2,0:T(8,128)S(1)} %fusion, bf16[448,16,152]{2,1,0:T(8,128)(2,1)} %copy.24, bf16[448,2,152,21]{2,3,0,1:T(8,128)(2,1)S(1)} %copy-done.1), kind=kOutput, calls=%fused_computation.6 | convolution fusion | flops 45911040 | bytes 11956224 | tf_op jit(solution)/shard_map/krs,ksq->kqr/dot_general | solution.py:33
  183.6 3.0 %copy.29 = f32[1,448,21,16]{1,3,2,0:T(8,128)S(1)} copy(f32[1,448,21,16]{2,3,1,0:T(8,128)} %add_bitcast_fusion) | data formatting | bytes 1204224 | tf_op jit(solution)/shard_map/stack | solution.py:37
  186.6 0.0 copy-start.2
  186.6 5.3 %fusion.1 = f32[448,21,16]{1,2,0:T(8,128)S(1)} fusion(bf16[448,16,152]{2,1,0:T(8,128)(2,1)} %copy.24, bf16[448,2,152,21]{2,3,0,1:T(8,128)(2,1)} %all-gather.2.cloned.1.call-done), kind=kOutput, calls=%fused_computation.3 | convolution fusion | flops 45760512 | bytes 9777152 | tf_op jit(solution)/shard_map/krs,ksq->kqr/dot_general | solution.py:33
  192.0 0.0 copy-done.2
  192.0 6.1 %subtract_bitcast_fusion = f32[1,448,21,16]{2,3,1,0:T(8,128)} fusion(f32[448,21,16]{1,2,0:T(8,128)S(1)} %fusion.1, bf16[448,16,152]{2,1,0:T(8,128)(2,1)S(1)} %copy-done.2, bf16[448,2,152,21]{2,3,0,1:T(8,128)(2,1)} %all-gather.2.cloned.1.call-done), kind=kOutput, calls=%fused_computation.7 | convolution fusion | flops 45911040 | bytes 8888320 | tf_op jit(solution)/shard_map/krs,ksq->kqr/dot_general | solution.py:33
  198.1 3.7 %copy.28 = f32[1,448,21,16]{1,3,2,0:T(8,128)} copy(f32[1,448,21,16]{2,3,1,0:T(8,128)} %subtract_bitcast_fusion) | data formatting | bytes 1204224 | tf_op jit(solution)/shard_map/stack | solution.py:37
  201.8 2.3 pad_maximum_fusion
  204.1 0.0 collective-permute-start
  204.1 2.0 fusion.10
  206.1 0.0 copy-start.4
  206.2 0.0 copy-start.5
  206.2 0.0 copy-start.6
  206.2 1.4 collective-permute-done
  207.6 0.0 copy-done.3
  207.6 2.7 fusion.60
  210.3 1.5 collective-permute-start.1
  211.8 0.0 copy-done.4
  211.8 0.0 copy-done.5
  211.8 0.2 select_reduce_fusion
  212.0 1.9 fusion.17
  213.9 0.1 copy.35
  214.0 0.1 convolution_bitcast_fusion
  214.1 61.0 %psum.7 = f32[21]{0:T(128)} all-reduce(f32[21]{0:T(128)S(1)} %convolution_bitcast_fusion), channel_id=1, replica_groups=mesh['freq'=8,'sens'=4] {'freq','sens'}, use_global_device_ids=true, to_apply=%region_1.2 | all-reduce | flops 21 | bytes 168 | tf_op jit(solution)/shard_map/psum | solution.py:69
  275.2 0.0 copy-done.6
  275.2 0.3 fusion.39
  275.5 3.6 %fusion.31 = (f32[1,448,420]{1,2,0:T(8,128)S(1)}, f32[1,448,420]{1,2,0:T(8,128)S(1)}) fusion(f32[448]{0:T(512)S(1)} %select_multiply_fusion, f32[448]{0:T(512)S(1)} %fusion.42), kind=kLoop, calls=%fused_computation.43 | loop fusion | flops 2069760 | bytes 1508864 | tf_op jit(solution)/shard_map/mul | solution.py:26
  279.1 0.0 collective-permute-done.1
  279.1 2.4 fusion.66
  281.5 0.2 multiply_subtract_fusion
  281.7 0.2 pad_maximum_fusion.1
  281.9 3.4 %fusion.19 = bf16[16,21,420]{2,1,0:T(8,128)(2,1)S(1)} fusion(f32[2,448,21,16]{1,3,2,0:T(8,128)S(1)} %pad_maximum_fusion.1, f32[1,448,420]{1,2,0:T(8,128)S(1)} %get-tuple-element.19, f32[1,448,420]{1,2,0:T(8,128)S(1)} %get-tuple-element.18), kind=kOutput, calls=%fused_computation.29 | convolution fusion | flops 1517839616 | bytes 2991744 | tf_op jit(solution)/shard_map/ckqr,ckt->rqt/dot_general | solution.py:82
  285.3 0.8 copy.31
  (3 shorter events, 0.0 us)
Async XLA Ops:
  7.2 8.2 %copy-start = (bf16[16,152,420]{2,1,0:T(8,128)(2,1)S(1)}, bf16[16,152,420]{2,1,0:T(8,128)(2,1)}, u32[]{:S(2)}) copy-start(bf16[16,152,420]{2,1,0:T(8,128)(2,1)} %param.5) | copy-start | bytes 6128644
  7.2 164.2 %all-gather.2.cloned.1.call-start = ((), (), s32[]{:S(2)}) async-start(), calls=%async_computation | async-start | bytes 12386304 | tf_op jit(solution)/shard_map/all_gather | solution.py:74
  171.4 6.8 %copy-start.1 = (bf16[448,2,152,21]{2,3,0,1:T(8,128)(2,1)S(1)}, bf16[448,2,152,21]{2,3,0,1:T(8,128)(2,1)}, u32[]{:S(2)}) copy-start(bf16[448,2,152,21]{2,3,0,1:T(8,128)(2,1)} %all-gather.2.cloned.1.call-done) | copy-start | bytes 17160196
  186.6 5.4 %copy-start.2 = (bf16[448,16,152]{2,1,0:T(8,128)(2,1)S(1)}, bf16[448,16,152]{2,1,0:T(8,128)(2,1)}, u32[]{:S(2)}) copy-start(bf16[448,16,152]{2,1,0:T(8,128)(2,1)} %copy.25) | copy-start | bytes 6537220
  204.1 3.5 %collective-permute-start = (f32[2,448,21,16]{1,3,2,0:T(8,128)}, f32[2,448,21,16]{1,3,2,0:T(8,128)}, u32[]{:S(2)}, u32[]{:S(2)}) collective-permute-start(f32[2,448,21,16]{1,3,2,0:T(8,128)} %pad_maximum_fusion), channel_id=1, source_target_pairs={{0,1},{1,0},{2,3},{3,2},{4,5},{5,4},{6,7},{7,6},{8,9},{9,8},{10,11... | collective-permute-start | bytes 3612680 | tf_op jit(solution)/shard_map/ppermute | solution.py:80
  204.1 3.5 %copy-start.3 = (f32[1,448,21,16]{1,3,2,0:T(8,128)S(1)}, f32[1,448,21,16]{1,3,2,0:T(8,128)}, u32[]{:S(2)}) copy-start(f32[1,448,21,16]{1,3,2,0:T(8,128)} %copy.28) | copy-start | bytes 1806340
  206.1 5.7 %copy-start.4 = (f32[600]{0:T(1024)S(1)}, f32[600]{0:T(1024)}, u32[]{:S(2)}) copy-start(f32[600]{0:T(1024)} %param.8) | copy-start | bytes 7204
  206.2 5.7 %copy-start.5 = (s32[152]{0:T(256)S(1)}, s32[152]{0:T(256)}, u32[]{:S(2)}) copy-start(s32[152]{0:T(256)} %param.7) | copy-start | bytes 1828
  206.2 69.0 %copy-start.6 = (s32[21]{0:T(128)S(1)}, s32[21]{0:T(128)}, u32[]{:S(2)}) copy-start(s32[21]{0:T(128)} %param.9) | copy-start | bytes 256
  210.3 68.8 %collective-permute-start.1 = (f32[2,448,21,16]{1,3,2,0:T(8,128)}, f32[2,448,21,16]{1,3,2,0:T(8,128)}, u32[]{:S(2)}, u32[]{:S(2)}) collective-permute-start(f32[2,448,21,16]{1,3,2,0:T(8,128)} %fusion.60), channel_id=1, source_target_pairs={{0,2},{1,3},{2,0},{3,1},{4,6},{5,7},{6,4},{7,5},{8,10},{9,11},{10,... | collective-permute-start | bytes 3612680 | tf_op jit(solution)/shard_map/ppermute | solution.py:80
Sparse Core Ops, SparseCore 0:
  11.7 159.6 all-gather.1
